TPU v7x, 32 devices: a whole 2x2x4 slice. The times are simulated.
32 devices in a mesh: pix: 8 (over z, x), band: 4 (over y, core).
Axes of the slice: x: 2, y: 2, z: 4, core: 2. Of those that a mesh axis runs over, the one named last changes fastest.
Arguments:
- spectra: bfloat16 [224, 32768], P('band', 'pix'), may hold values from -0.1 to 4
- endmembers: bfloat16 [224, 512], P('band'), may hold values from 0.05 to 1
- gram_inverse: float32 [512, 512], replicated, may hold values from -1 to 1, as said below
- abundances: float32 [512, 32768], P(None, ('pix', 'band')), may hold values from 0 to 512, as said below
- duals: float32 [512, 32768], P(None, ('pix', 'band')), may hold values from -4 to 4
Outputs:
- abundances_out: float32 [512, 32768], P(None, ('pix', 'band'))
- duals_out: float32 [512, 32768], P(None, ('pix', 'band'))
- residual_rms: float32 [2, 2], replicated
Inputs may be any that keep to these rules, and one draw needn't show every extreme that they name: `abundances`: each column is nonnegative and sums to 512. `gram_inverse`: penalty times the float32 inverse of endmembers^T endmembers / 512^2 + penalty I, with penalty = 224 / (2 * 512^2) and the endmembers as stored.
All inputs are finite; a program needn't handle non-finite values.
Results may differ from a plain program's by a relative error of at most 0.0004.
Values may be sent and summed in bfloat16 or wider, within the bound.
No kernel may reach another device: no remote copies, remote signals or barrier semaphores. Data moves between devices by JAX's collectives and lax.ppermute only.
A program may use at most 64 MiB of HBM per device.

v0:
```python
import jax
import jax.numpy as jnp
from jax import lax
from jax.sharding import PartitionSpec as P

B = 224
K = 512
ITERS = 2
BISECT = 6


def project(shifted):
    simplex_sum = float(K)
    high_end = jnp.max(shifted, axis=0)
    low_end = (jnp.sum(shifted, axis=0) - simplex_sum) / simplex_sum

    def mass_at(level):
        return jnp.sum(jnp.maximum(shifted - level[None, :], 0.0), axis=0)

    mass_low = mass_at(low_end)
    mass_high = jnp.zeros_like(high_end)

    def bisect_once(unused, state):
        low_now, high_now, low_mass, high_mass = state
        middle = 0.5 * (low_now + high_now)
        total_mass = mass_at(middle)
        too_high = total_mass > simplex_sum
        return (
            jnp.where(too_high, middle, low_now),
            jnp.where(too_high, high_now, middle),
            jnp.where(too_high, total_mass, low_mass),
            jnp.where(too_high, high_mass, total_mass),
        )

    low_end, high_end, mass_low, mass_high = lax.fori_loop(
        0, BISECT, bisect_once, (low_end, high_end, mass_low, mass_high)
    )
    level = low_end + (mass_low - simplex_sum) * (high_end - low_end) / (mass_low - mass_high)
    return jnp.maximum(shifted - level[None, :], 0.0)


def contract_bands(signatures, columns):
    return lax.dot_general(
        signatures, columns, (((0,), (0,)), ((), ())), preferred_element_type=jnp.float32
    )


def body(spectra, endmembers, gram_inverse, abundances, duals):
    penalty = B / (2.0 * K * K)
    exchanged = lax.all_to_all(spectra, "band", split_axis=1, concat_axis=0, tiled=True)
    all_rows = lax.all_gather(endmembers, "band", axis=0, tiled=True)
    fit_term = contract_bands(all_rows, exchanged)
    fit_term = fit_term / K
    pixel_count = abundances.shape[1] * lax.axis_size("pix") * lax.axis_size("band")
    current = abundances
    scaled_dual = duals
    primal_list = []
    change_list = []
    for sweep in range(ITERS):
        primal = jnp.dot(
            gram_inverse,
            fit_term / penalty + current - scaled_dual,
            precision=lax.Precision.HIGHEST,
        )
        updated = project(primal + scaled_dual)
        scaled_dual = scaled_dual + primal - updated
        primal_sum = jnp.sum((primal - updated) ** 2)
        change_sum = jnp.sum((updated - current) ** 2)
        primal_sum, change_sum = lax.psum((primal_sum, change_sum), ("pix", "band"))
        primal_list.append(primal_sum)
        change_list.append(change_sum)
        current = updated
    totals = jnp.stack([jnp.stack(primal_list), jnp.stack(change_list)])
    residual_rms = jnp.sqrt(totals / pixel_count)
    return (current, scaled_dual, residual_rms)


def solution(mesh):
    return jax.shard_map(
        body,
        mesh=mesh,
        in_specs=(
            P("band", "pix"),
            P("band", None),
            P(),
            P(None, ("pix", "band")),
            P(None, ("pix", "band")),
        ),
        out_specs=(P(None, ("pix", "band")), P(None, ("pix", "band")), P()),
        check_vma=False,
    )
```

profile of v0, /device:TPU:0, one launch (start us, length us, event | category | flops | bytes accessed | tf_op | source)
XLA Modules:
  0.0 99.4 jit_solution(1292467306230520806)
XLA Ops:
  0.6 0.0 copy-start
  0.6 1.9 %copy.12 = bf16[7,4,8,1024]{3,2,0,1:T(8,128)(2,1)} copy(bf16[7,4,8,1024]{3,2,1,0:T(8,128)(2,1)} %bitcast.36) | data formatting | bytes 917504 | tf_op jit(solution)/shard_map/all_to_all | solution.py:50
  2.5 4.3 %all-to-all-start = ((bf16[56,4,1024]{2,0,1:T(8,128)(2,1)}), bf16[56,4,1024]{2,0,1:T(8,128)(2,1)S(1)}, u32[]{:S(2)}, u32[]{:S(2)}) async-start(bf16[56,4,1024]{2,0,1:T(8,128)(2,1)} %bitcast.34), calls=%async_computation | async-start | bytes 917504 | tf_op jit(solution)/shard_map/all_to_all | solution.py:50
  6.8 10.2 %all_gather.3 = bf16[224,512]{1,0:T(8,128)(2,1)S(1)} all-gather(bf16[56,512]{1,0:T(8,128)(2,1)} %param.10), channel_id=1, replica_groups=mesh['pix'=8,'band'=4] {'band'}, dimensions={0}, use_global_device_ids=true | all-gather | bytes 286720 | tf_op jit(solution)/shard_map/all_gather | solution.py:51
  17.0 0.0 all-to-all-done
  17.0 0.5 fusion.30
  17.5 0.0 copy-start.4
  17.5 8.7 %fusion.29 = (f32[1024]{0:T(1024)S(1)}, f32[512,1024]{1,0:T(8,128)S(1)}, f32[1024,512]{0,1:T(8,128)}) fusion(f32[512,1024]{1,0:T(8,128)} %param.13, f32[512,512]{1,0:T(8,128)S(1)} %copy-done, f32[512,1024]{1,0:T(8,128)} %param.12, f32[512,1024]{1,0:T(8,128)S(1)} %fusion.30), kind=kOutput, calls=%fused_computation.54 | convolution fusion | flops 3223845888 | bytes 11538432 | tf_op jit(solution)/shard_map/dot_general | solution.py:60
  26.2 0.3 maximum_reduce_fusion.3
  26.5 1.9 %while.34 = (s32[]{:T(128)}, f32[1024]{0:T(1024)S(1)}, f32[1024]{0:T(1024)S(1)}, f32[1024]{0:T(1024)S(1)}, f32[1024]{0:T(1024)S(1)}, /*index=5*/f32[512,1024]{1,0:T(8,128)S(1)}, s32[]{:T(128)}, s32[]{:T(128)}) while((s32[]{:T(128)}, f32[1024]{0:T(1024)S(1)}, f32[1024]{0:T(1024)S(1)}, f32[1024]{0:T(1024)S(1)}, f32[1024]{0:T(1024)S(1)}, ...), condition=%wide.region_5.6_spmd.clone, body=%wide.region_3.5_spmd.clone.sunk | while | flops 1582083 | bytes 2154591 | solution.py:35
  26.5 0.3 maximum_reduce_fusion.6
  26.9 0.3 maximum_reduce_fusion.6
  27.2 0.3 maximum_reduce_fusion.6
  27.5 0.3 maximum_reduce_fusion.6
  27.8 0.3 maximum_reduce_fusion.6
  28.1 0.3 maximum_reduce_fusion.6
  28.4 7.0 %fusion.28 = (f32[1024]{0:T(1024)S(1)}, f32[512,1024]{1,0:T(8,128)S(1)}, f32[1024,512]{0,1:T(8,128)}) fusion(f32[512,1024]{1,0:T(8,128)S(1)} %get-tuple-element.314, f32[1024]{0:T(1024)S(1)} %divide_add_fusion.1, f32[512,512]{1,0:T(8,128)S(1)} %copy-done, f32[512,1024]{1,0:T(8,128)} %copy-done.4), kind=kOutput, calls=%fused_computation.53 | convolution fusion | flops 3226991616 | bytes 9445376 | tf_op jit(solution)/shard_map/dot_general | solution.py:60
  35.5 0.3 maximum_reduce_fusion.2
  35.8 0.9 copy-done.1
  36.8 11.3 %while.35 = (s32[]{:T(128)}, f32[1024]{0:T(1024)S(1)}, f32[1024]{0:T(1024)S(1)}, f32[1024]{0:T(1024)S(1)}, f32[1024]{0:T(1024)S(1)}, /*index=5*/f32[512,1024]{1,0:T(8,128)}, s32[]{:T(128)}, s32[]{:T(128)}) while((s32[]{:T(128)}, f32[1024]{0:T(1024)S(1)}, f32[1024]{0:T(1024)S(1)}, f32[1024]{0:T(1024)S(1)}, f32[1024]{0:T(1024)S(1)}, ...), condition=%wide.region_11.12_spmd.clone, body=%wide.region_9.0_spmd.clone.sunk | while | flops 1582083 | bytes 2154591 | solution.py:35
  36.8 1.8 %maximum_reduce_fusion.7 = f32[1024]{0:T(1024)S(1)} fusion(f32[512,1024]{1,0:T(8,128)} %get-tuple-element.311, f32[1024]{0:T(1024)S(1)} %add_multiply_fusion.7), kind=kLoop, calls=%fused_computation.7.clone.1 | loop fusion | flops 1571840 | bytes 2105344 | tf_op jit(solution)/shard_map/while/body/eval_jaxpr/reduce_sum | solution.py:18
  38.7 1.8 %maximum_reduce_fusion.7 = f32[1024]{0:T(1024)S(1)} fusion(f32[512,1024]{1,0:T(8,128)} %get-tuple-element.311, f32[1024]{0:T(1024)S(1)} %add_multiply_fusion.7), kind=kLoop, calls=%fused_computation.7.clone.1 | loop fusion | flops 1571840 | bytes 2105344 | tf_op jit(solution)/shard_map/while/body/eval_jaxpr/reduce_sum | solution.py:18
  40.5 1.8 %maximum_reduce_fusion.7 = f32[1024]{0:T(1024)S(1)} fusion(f32[512,1024]{1,0:T(8,128)} %get-tuple-element.311, f32[1024]{0:T(1024)S(1)} %add_multiply_fusion.7), kind=kLoop, calls=%fused_computation.7.clone.1 | loop fusion | flops 1571840 | bytes 2105344 | tf_op jit(solution)/shard_map/while/body/eval_jaxpr/reduce_sum | solution.py:18
  42.4 1.8 %maximum_reduce_fusion.7 = f32[1024]{0:T(1024)S(1)} fusion(f32[512,1024]{1,0:T(8,128)} %get-tuple-element.311, f32[1024]{0:T(1024)S(1)} %add_multiply_fusion.7), kind=kLoop, calls=%fused_computation.7.clone.1 | loop fusion | flops 1571840 | bytes 2105344 | tf_op jit(solution)/shard_map/while/body/eval_jaxpr/reduce_sum | solution.py:18
  44.3 1.8 %maximum_reduce_fusion.7 = f32[1024]{0:T(1024)S(1)} fusion(f32[512,1024]{1,0:T(8,128)} %get-tuple-element.311, f32[1024]{0:T(1024)S(1)} %add_multiply_fusion.7), kind=kLoop, calls=%fused_computation.7.clone.1 | loop fusion | flops 1571840 | bytes 2105344 | tf_op jit(solution)/shard_map/while/body/eval_jaxpr/reduce_sum | solution.py:18
  46.2 1.8 %maximum_reduce_fusion.7 = f32[1024]{0:T(1024)S(1)} fusion(f32[512,1024]{1,0:T(8,128)} %get-tuple-element.311, f32[1024]{0:T(1024)S(1)} %add_multiply_fusion.7), kind=kLoop, calls=%fused_computation.7.clone.1 | loop fusion | flops 1571840 | bytes 2105344 | tf_op jit(solution)/shard_map/while/body/eval_jaxpr/reduce_sum | solution.py:18
  48.1 5.6 %fusion.9 = (f32[]{:T(128)}, f32[]{:T(128)}, f32[]{:T(128)}, f32[]{:T(128)}, f32[512,1024]{1,0:T(8,128)S(1)}) fusion(f32[1024,512]{0,1:T(8,128)} %get-tuple-element.172, f32[512,1024]{1,0:T(8,128)S(1)} %get-tuple-element.314, f32[1024]{0:T(1024)S(1)} %divide_add_fusion.1, f32[512,1024]{1,0:T(8,128)} %param.12, f32[1024,512]{0,1:T(8,128)} %get-tuple-element.173, ...), kind=kLoop, calls=%fused_computation.21 | loop fusion | flops 8388604 | bytes 12591120 | tf_op jit(solution)/shard_map/reduce_sum | solution.py:67
  53.7 2.0 %sub.115 = f32[512,1024]{1,0:T(8,128)} subtract(f32[512,1024]{1,0:T(8,128)S(1)} %copy-done.2, f32[512,1024]{1,0:T(8,128)S(1)} %get-tuple-element.159) | non-fusion elementwise | flops 524288 | bytes 6291456 | tf_op jit(solution)/shard_map/sub | solution.py:66
  55.7 0.0 copy-done.3
  55.7 40.5 %all-reduce = (f32[1]{0:T(128)}, f32[1]{0:T(128)}, f32[1]{0:T(128)}, f32[1]{0:T(128)}) all-reduce(f32[1]{0:T(128)} %bitcast.8, f32[1]{0:T(128)} %bitcast.7, f32[1]{0:T(128)} %bitcast.5, f32[1]{0:T(128)} %bitcast.4), channel_id=1, replica_groups=mesh['pix'=8,'band'=4] {'pix','band'}, use_global_device_ids=true, to_apply=%region_19.20 | all-reduce | flops 4 | bytes 32 | tf_op jit(solution)/shard_map/psum | solution.py:69
  96.2 2.6 %maximum_bitcast_fusion = (f32[1,2]{1,0:T(1,128)S(1)}, f32[1,2]{1,0:T(1,128)S(1)}) fusion(f32[1]{0:T(128)} %get-tuple-element.157, f32[1]{0:T(128)} %get-tuple-element.158, f32[1]{0:T(128)} %get-tuple-element.155, f32[1]{0:T(128)} %get-tuple-element.156), kind=kLoop, calls=%fused_computation.48 | loop fusion | flops 4 | bytes 32 | tf_op jit(solution)/shard_map/stack | solution.py:73
  98.8 0.6 fusion.24
  (36 shorter events, 0.2 us)
Async XLA Ops:
  0.6 16.8 %copy-start = (f32[512,512]{1,0:T(8,128)S(1)}, f32[512,512]{1,0:T(8,128)}, u32[]{:S(2)}) copy-start(f32[512,512]{1,0:T(8,128)} %param.11) | copy-start | bytes 3145732
  2.5 14.4 %all-to-all-start = ((bf16[56,4,1024]{2,0,1:T(8,128)(2,1)}), bf16[56,4,1024]{2,0,1:T(8,128)(2,1)S(1)}, u32[]{:S(2)}, u32[]{:S(2)}) async-start(bf16[56,4,1024]{2,0,1:T(8,128)(2,1)} %bitcast.34), calls=%async_computation | async-start | bytes 917504 | tf_op jit(solution)/shard_map/all_to_all | solution.py:50
  17.5 8.7 %copy-start.4 = (f32[512,1024]{1,0:T(8,128)}, f32[512,1024]{1,0:T(8,128)S(1)}, u32[]{:S(2)}) copy-start(f32[512,1024]{1,0:T(8,128)S(1)} %fusion.30) | copy-start | bytes 6291460
  35.5 1.3 %copy-start.1 = (f32[512,1024]{1,0:T(8,128)}, f32[512,1024]{1,0:T(8,128)S(1)}, u32[]{:S(2)}) copy-start(f32[512,1024]{1,0:T(8,128)S(1)} %get-tuple-element.295) | copy-start | bytes 6291460
  48.1 5.6 %copy-start.2 = (f32[512,1024]{1,0:T(8,128)S(1)}, f32[512,1024]{1,0:T(8,128)}, u32[]{:S(2)}) copy-start(f32[512,1024]{1,0:T(8,128)} %get-tuple-element.315) | copy-start | bytes 6291460
  53.7 2.0 %copy-start.3 = (f32[512,1024]{1,0:T(8,128)}, f32[512,1024]{1,0:T(8,128)S(1)}, u32[]{:S(2)}) copy-start(f32[512,1024]{1,0:T(8,128)S(1)} %get-tuple-element.159) | copy-start | bytes 6291460
where the time goes:
time: 99.9 us; the launch traced here: 99.4 us
  blocking collectives  50.7 us (51%)
  other arithmetic  24.3 us (24%)
  matrix products  16.2 us (16%)
  starting transfers between devices  4.26 us (4%)
  local copies, waits for them, and re-layouts  2.88 us (3%)
    psum x1, blocking collectives, body(): primal_sum, change_sum = lax.psum((primal_sum, change_sum), ('pix', 'band'))  40.5 us
    dot_general x2, matrix products, body(): jnp.dot(gram_inverse, fit_term / penalty + current - scaled_dual, precisi...  15.7 us
    reduce_sum x14, other arithmetic, mass_at(): return jnp.sum(jnp.maximum(shifted - level[None, :], 0.0), axis=0)  13.3 us
    all_gather x1, blocking collectives, body(): all_rows = lax.all_gather(endmembers, 'band', axis=0, tiled=True)  10.2 us
    reduce_sum x1, other arithmetic, body(): primal_sum = jnp.sum((primal - updated) ** 2)  5.61 us
    all_to_all x1, starting transfers between devices, body(): lax.all_to_all(spectra, 'band', split_axis=1, concat_axis=0, tiled=True)  4.26 us
    another operation x1, other arithmetic, body(): totals = jnp.stack([jnp.stack(primal_list), jnp.stack(change_list)])  2.6 us
    sub x1, other arithmetic, body(): scaled_dual = scaled_dual + primal - updated  2 us
  transfers between devices with their start and end apart: 1, of which 0 were waited for; matrix products, arithmetic and copies ran while one was open for 0% of the time, Pallas kernels for 0%

commit v1 on v0

--- a/solution.py
+++ b/solution.py
@@ -47,7 +47,10 @@
 
 def body(spectra, endmembers, gram_inverse, abundances, duals):
     penalty = B / (2.0 * K * K)
-    exchanged = lax.all_to_all(spectra, "band", split_axis=1, concat_axis=0, tiled=True)
+    exchanged = jnp.concatenate(
+        lax.all_to_all(jnp.stack(jnp.split(spectra, lax.axis_size("band"), axis=1)), "band", 0, 0),
+        axis=0,
+    )
     all_rows = lax.all_gather(endmembers, "band", axis=0, tiled=True)
     fit_term = contract_bands(all_rows, exchanged)
     fit_term = fit_term / K

time: 99.9 us -> 104 us (1.041)
  local copies, waits for them, and re-layouts: 2.88 us -> 15.4 us
  other arithmetic: 24.3 us -> 18.3 us
  blocking collectives: 50.7 us -> 48.3 us
    unnamed x10 -> x16, local copies, waits for them, and re-layouts: 0.98 us -> 14.2 us
    reduce_sum x14, other arithmetic: 13.3 us -> 7.65 us  [mass_at(): return jnp.sum(jnp.maximum(shifted - level[None, :], 0.0), axis=0)]
    all_gather x1, blocking collectives: 10.2 us -> 6.93 us  [body(): all_rows = lax.all_gather(endmembers, 'band', axis=0, tiled=True)]
    sub x1 -> x0, other arithmetic: 2 us -> none  [body(): scaled_dual = scaled_dual + primal - updated]
    all_to_all x1 -> x0, local copies, waits for them, and re-layouts: 1.9 us -> none  [body(): lax.all_to_all(spectra, 'band', split_axis=1, concat_axis=0, tiled=True)]
    dot_general x2, matrix products: 15.7 us -> 14.1 us  [body(): jnp.dot(gram_inverse, fit_term / penalty + current - scaled_dual, precisi...]
    another operation x0 -> x1, local copies, waits for them, and re-layouts: none -> 1.19 us  [body(): jnp.stack(jnp.split(spectra, lax.axis_size('band'), axis=1))]
    dot_general x1, matrix products: 0.47 us -> 1.64 us  [contract_bands(): lax.dot_general(signatures, columns, (((0,), (0,)), ((), ())), preferred_...]
  transfers between devices with their start and end apart: 1 -> 1, of which waited for: 0 -> 0; matrix products, arithmetic and copies ran while one was open for 0% -> 5% of each run, Pallas kernels for 0% -> 0%
where the time goes in v1:
time: 104 us; the launch traced here: 103 us
  blocking collectives  48.3 us (46%)
  other arithmetic  18.3 us (18%)
  matrix products  15.7 us (15%)
  local copies, waits for them, and re-layouts  15.4 us (15%)
  starting transfers between devices  4.26 us (4%)
    psum x1, blocking collectives, body(): primal_sum, change_sum = lax.psum((primal_sum, change_sum), ('pix', 'band'))  41.4 us
    unnamed x16, local copies, waits for them, and re-layouts  14.2 us
    dot_general x2, matrix products, body(): jnp.dot(gram_inverse, fit_term / penalty + current - scaled_dual, precisi...  14.1 us
    reduce_sum x14, other arithmetic, mass_at(): return jnp.sum(jnp.maximum(shifted - level[None, :], 0.0), axis=0)  7.65 us
    all_gather x1, blocking collectives, body(): all_rows = lax.all_gather(endmembers, 'band', axis=0, tiled=True)  6.93 us
    reduce_sum x1, other arithmetic, body(): primal_sum = jnp.sum((primal - updated) ** 2)  6.42 us
    all_to_all x1, starting transfers between devices, body(): lax.all_to_all(jnp.stack(jnp.split(spectra, lax.axis_size('band'), axis=1...  4.26 us
    another operation x1, other arithmetic, body(): totals = jnp.stack([jnp.stack(primal_list), jnp.stack(change_list)])  2.6 us
  transfers between devices with their start and end apart: 1, of which 0 were waited for; matrix products, arithmetic and copies ran while one was open for 5% of the time, Pallas kernels for 0%

profile of v1, /device:TPU:0, one launch (start us, length us, event | category | flops | bytes accessed | tf_op | source)
XLA Modules:
  0.0 103.1 jit_solution(4919223918417186719)
XLA Ops:
  0.6 1.2 %slice_bitcast_fusion.3 = (bf16[1,56,1024]{2,1,0:T(8,128)(2,1)S(1)}, bf16[1,56,1024]{2,1,0:T(8,128)(2,1)S(1)}, bf16[1,56,1024]{2,1,0:T(8,128)(2,1)S(1)}, bf16[1,56,1024]{2,1,0:T(8,128)(2,1)S(1)}) fusion(bf16[56,4096]{1,0:T(8,128)(2,1)} %param.9), kind=kLoop, calls=%fused_computation.45 | loop fusion | bytes 917504 | tf_op jit(solution)/shard_map/stack | solution.py:51
  1.8 0.8 pad_maximum_fusion
  2.7 4.3 %all-to-all-start = ((bf16[4,56,1024]{2,1,0:T(8,128)(2,1)}), bf16[4,56,1024]{2,1,0:T(8,128)(2,1)}, u32[]{:S(2)}, u32[]{:S(2)}) async-start(bf16[4,56,1024]{2,1,0:T(8,128)(2,1)} %pad_maximum_fusion), calls=%async_computation | async-start | bytes 917504 | tf_op jit(solution)/shard_map/all_to_all | solution.py:51
  6.9 1.9 %copy.8 = f32[512,1024]{0,1:T(8,128)S(1)} copy(f32[512,1024]{1,0:T(8,128)} %param.12) | data formatting | bytes 4194304 | tf_op args[3]
  8.9 3.7 %copy.9 = f32[512,1024]{0,1:T(8,128)} copy(f32[512,1024]{1,0:T(8,128)} %param.13) | data formatting | bytes 4194304 | tf_op args[4]
  12.5 6.9 %all_gather.3 = bf16[224,512]{1,0:T(8,128)(2,1)S(1)} all-gather(bf16[56,512]{1,0:T(8,128)(2,1)S(1)} %copy-done.4), channel_id=1, replica_groups=mesh['pix'=8,'band'=4] {'band'}, dimensions={0}, use_global_device_ids=true | all-gather | bytes 286720 | tf_op jit(solution)/shard_map/all_gather | solution.py:54
  19.5 1.6 %fusion.31 = f32[1024,512]{1,0:T(8,128)S(1)} fusion(bf16[224,1024]{1,0:T(8,128)(2,1)} %bitcast.4, bf16[224,512]{1,0:T(8,128)(2,1)S(1)} %all_gather.3), kind=kOutput, calls=%fused_computation.60 | convolution fusion | flops 234881024 | bytes 2785280 | tf_op jit(solution)/shard_map/dot_general | solution.py:43
  21.2 5.2 %fusion.30 = (f32[1024]{0:T(1024)S(1)}, f32[512,1024]{0,1:T(8,128)}, f32[1024,512]{1,0:T(8,128)}) fusion(f32[512,1024]{0,1:T(8,128)S(1)} %copy-done.3, f32[512,512]{1,0:T(8,128)S(1)} %copy-done, f32[512,1024]{0,1:T(8,128)S(1)} %copy.8, f32[1024,512]{1,0:T(8,128)S(1)} %fusion.31), kind=kOutput, calls=%fused_computation.59 | convolution fusion | flops 3223845888 | bytes 11538432 | tf_op jit(solution)/shard_map/dot_general | solution.py:63
  26.5 1.9 %copy.12 = f32[512,1024]{1,0:T(8,128)S(1)} copy(f32[512,1024]{0,1:T(8,128)} %get-tuple-element.177) | data formatting | bytes 4194304
  28.4 2.2 %maximum_reduce_fusion.3 = (f32[1024]{0:T(1024)S(1)}, f32[1024]{0:T(1024)S(1)}) fusion(f32[512,1024]{0,1:T(8,128)} %get-tuple-element.177, f32[1024]{0:T(1024)S(1)} %add_multiply_fusion.3), kind=kLoop, calls=%fused_computation.34 | loop fusion | flops 2095104 | bytes 2109440 | tf_op jit(solution)/shard_map/reduce_sum | solution.py:18
  30.6 1.9 %while.34 = (s32[]{:T(128)}, f32[1024]{0:T(1024)S(1)}, f32[1024]{0:T(1024)S(1)}, f32[1024]{0:T(1024)S(1)}, f32[1024]{0:T(1024)S(1)}, /*index=5*/f32[512,1024]{1,0:T(8,128)S(1)}, s32[]{:T(128)}, s32[]{:T(128)}) while((s32[]{:T(128)}, f32[1024]{0:T(1024)S(1)}, f32[1024]{0:T(1024)S(1)}, f32[1024]{0:T(1024)S(1)}, f32[1024]{0:T(1024)S(1)}, ...), condition=%wide.region_5.6_spmd.clone, body=%wide.region_3.5_spmd.clone.sunk | while | flops 1582083 | bytes 2154591 | solution.py:35
  30.6 0.3 maximum_reduce_fusion.6
  30.9 0.3 maximum_reduce_fusion.6
  31.2 0.3 maximum_reduce_fusion.6
  31.5 0.3 maximum_reduce_fusion.6
  31.9 0.3 maximum_reduce_fusion.6
  32.2 0.3 maximum_reduce_fusion.6
  32.5 8.9 %fusion.29 = (f32[1024]{0:T(1024)S(1)}, f32[512,1024]{0,1:T(8,128)}, f32[1024,512]{1,0:T(8,128)}) fusion(f32[512,1024]{0,1:T(8,128)} %get-tuple-element.177, f32[1024]{0:T(1024)S(1)} %divide_add_fusion.1, f32[512,512]{1,0:T(8,128)S(1)} %copy-done, f32[1024,512]{1,0:T(8,128)} %copy-done.2), kind=kOutput, calls=%fused_computation.58 | convolution fusion | flops 3226991616 | bytes 9445376 | tf_op jit(solution)/shard_map/dot_general | solution.py:63
  41.3 1.9 %copy.14 = f32[512,1024]{1,0:T(8,128)S(1)} copy(f32[512,1024]{0,1:T(8,128)} %get-tuple-element.175) | data formatting | bytes 4194304
  43.3 2.2 %maximum_reduce_fusion.2 = (f32[1024]{0:T(1024)S(1)}, f32[1024]{0:T(1024)S(1)}) fusion(f32[512,1024]{0,1:T(8,128)} %get-tuple-element.175, f32[1024]{0:T(1024)S(1)} %add_multiply_fusion.2), kind=kLoop, calls=%fused_computation.31 | loop fusion | flops 2095104 | bytes 2109440 | tf_op jit(solution)/shard_map/reduce_sum | solution.py:18
  45.4 1.9 %while.35 = (s32[]{:T(128)}, f32[1024]{0:T(1024)S(1)}, f32[1024]{0:T(1024)S(1)}, f32[1024]{0:T(1024)S(1)}, f32[1024]{0:T(1024)S(1)}, /*index=5*/f32[512,1024]{1,0:T(8,128)S(1)}, s32[]{:T(128)}, s32[]{:T(128)}) while((s32[]{:T(128)}, f32[1024]{0:T(1024)S(1)}, f32[1024]{0:T(1024)S(1)}, f32[1024]{0:T(1024)S(1)}, ...), condition=%wide.region_11.12_spmd.clone, body=%wide.region_9.0_spmd.clone.sunk | while | flops 1582083 | bytes 2154591 | solution.py:35
  45.5 0.3 maximum_reduce_fusion.7
  45.8 0.3 maximum_reduce_fusion.7
  46.1 0.3 maximum_reduce_fusion.7
  46.4 0.3 maximum_reduce_fusion.7
  46.7 0.3 maximum_reduce_fusion.7
  47.4 6.4 %fusion.9 = (f32[]{:T(128)}, f32[]{:T(128)}, f32[]{:T(128)}, f32[]{:T(128)}, f32[512,1024]{0,1:T(8,128)}, /*index=5*/f32[512,1024]{0,1:T(8,128)S(1)}) fusion(f32[1024,512]{1,0:T(8,128)} %get-tuple-element.192, f32[512,1024]{0,1:T(8,128)} %get-tuple-element.177, f32[1024]{0:T(1024)S(1)} %divide_add_fusion.1, f32[512,1024]{0,1:T(8,128)} %copy-done.1, ...), kind=kLoop, calls=%fused_computation.21 | loop fusion | flops 8912892 | bytes 14688272 | tf_op jit(solution)/shard_map/reduce_sum | solution.py:70
  53.8 2.9 %copy.16 = f32[512,1024]{1,0:T(8,128)} copy(f32[512,1024]{0,1:T(8,128)} %get-tuple-element.186) | data formatting | bytes 4194304
  56.7 1.8 %copy.17 = f32[512,1024]{1,0:T(8,128)} copy(f32[512,1024]{0,1:T(8,128)S(1)} %get-tuple-element.187) | data formatting | bytes 4194304
  58.5 41.4 %all-reduce = (f32[1]{0:T(128)}, f32[1]{0:T(128)}, f32[1]{0:T(128)}, f32[1]{0:T(128)}) all-reduce(f32[1]{0:T(128)} %bitcast.12, f32[1]{0:T(128)} %bitcast.11, f32[1]{0:T(128)} %bitcast.9, f32[1]{0:T(128)} %bitcast.8), channel_id=1, replica_groups=mesh['pix'=8,'band'=4] {'pix','band'}, use_global_device_ids=true, to_apply=%region_19.20 | all-reduce | flops 4 | bytes 32 | tf_op jit(solution)/shard_map/psum | solution.py:72
  99.9 2.6 %maximum_bitcast_fusion = (f32[1,2]{1,0:T(1,128)S(1)}, f32[1,2]{1,0:T(1,128)S(1)}) fusion(f32[1]{0:T(128)} %get-tuple-element.172, f32[1]{0:T(128)} %get-tuple-element.173, f32[1]{0:T(128)} %get-tuple-element.170, f32[1]{0:T(128)} %get-tuple-element.171), kind=kLoop, calls=%fused_computation.52 | loop fusion | flops 4 | bytes 32 | tf_op jit(solution)/shard_map/stack | solution.py:76
  102.5 0.6 fusion.24
  (42 shorter events, 0.6 us)
Async XLA Ops:
  0.6 20.5 %copy-start = (f32[512,512]{1,0:T(8,128)S(1)}, f32[512,512]{1,0:T(8,128)}, u32[]{:S(2)}) copy-start(f32[512,512]{1,0:T(8,128)} %param.11) | copy-start | bytes 3145732
  2.7 16.8 %all-to-all-start = ((bf16[4,56,1024]{2,1,0:T(8,128)(2,1)}), bf16[4,56,1024]{2,1,0:T(8,128)(2,1)}, u32[]{:S(2)}, u32[]{:S(2)}) async-start(bf16[4,56,1024]{2,1,0:T(8,128)(2,1)} %pad_maximum_fusion), calls=%async_computation | async-start | bytes 917504 | tf_op jit(solution)/shard_map/all_to_all | solution.py:51
  8.9 12.3 %copy-start.1 = (f32[512,1024]{0,1:T(8,128)}, f32[512,1024]{0,1:T(8,128)S(1)}, u32[]{:S(2)}) copy-start(f32[512,1024]{0,1:T(8,128)S(1)} %copy.8) | copy-start | bytes 6291460
  8.9 3.7 %copy-start.4 = (bf16[56,512]{1,0:T(8,128)(2,1)S(1)}, bf16[56,512]{1,0:T(8,128)(2,1)}, u32[]{:S(2)}) copy-start(bf16[56,512]{1,0:T(8,128)(2,1)} %param.10) | copy-start | bytes 172036
  19.5 1.7 %copy-start.3 = (f32[512,1024]{0,1:T(8,128)S(1)}, f32[512,1024]{0,1:T(8,128)}, u32[]{:S(2)}) copy-start(f32[512,1024]{0,1:T(8,128)} %copy.9) | copy-start | bytes 6291460
  21.2 5.2 %copy-start.2 = (f32[1024,512]{1,0:T(8,128)}, f32[1024,512]{1,0:T(8,128)S(1)}, u32[]{:S(2)}) copy-start(f32[1024,512]{1,0:T(8,128)S(1)} %fusion.31) | copy-start | bytes 6291460
